TPU v7x, 32 devices: a whole 2x2x4 slice. The times are simulated.
32 devices in a mesh: ep: 8 (over z, x), dp: 4 (over y, core).
Axes of the slice: x: 2, y: 2, z: 4, core: 2. Of those that a mesh axis runs over, the one named last changes fastest.
Arguments:
- residual: bfloat16 [4096, 2880], P(('ep', 'dp')), may hold values from -400 to 400, as said below
- norm_gain: float32 [2880], replicated, may hold values from 0.25 to 1.75
- router_weight: bfloat16 [2880, 32], replicated, may hold values from -0.109375 to 0.109375
- out_grad: bfloat16 [4096, 2880], P(('ep', 'dp')), may hold values from -6 to 6
- expert_ids: int32 [4096, 4], P(('ep', 'dp')), may hold values from 0 to 31, all different within a row; in each aligned block of 128 rows (0 to 127, 128 to 255, ...) at most 24 rows name the same one
- hidden: bfloat16 [32, 768, 1440], P(('ep', 'dp')), may hold values from -0.3125 to 0.3125
- down_weight: bfloat16 [32, 1440, 2880], P(('ep', 'dp')), may hold values from -0.15625 to 0.15625
Outputs:
- hidden_grad: bfloat16 [32, 768, 1440], P(('ep', 'dp'))
- down_weight_grad: bfloat16 [32, 1440, 2880], P(('ep', 'dp'))
- residual_grad: bfloat16 [4096, 2880], P(('ep', 'dp'))
- router_grad: float32 [2880, 32], replicated
- gain_grad: float32 [2880], replicated
Inputs may be any that keep to these rules, and one draw needn't show every extreme that they name: `expert_ids`: in the tokens of one device no expert is named more than 24 times, a bound that some block reaches. `residual`: Real-valued entries.
All inputs are finite; a program needn't handle non-finite values.
Results may differ from a plain program's by a relative error of at most 0.0085.
Values may be sent and summed in bfloat16 or wider, within the bound.
A program may use at most 128 MiB of HBM per device.

v0:
```python
import functools
import math

import jax
import jax.numpy as jnp
from jax import lax
from jax.experimental import pallas as pl
from jax.experimental.pallas import tpu as pltpu
from jax.sharding import PartitionSpec as P

F32 = jnp.float32
BF16 = jnp.bfloat16
LINE = 4


def kernel(
    n_ep, n_dp, lines, cap,
    res_ref, gain_ref, rwt_ref, og_ref, ids_ref, hidt_any, w_any,
    hgt_any, wg_any, rg_ref, rgt_ref, gg_ref,
    tok, meta, metat, send, recv, w, hid3, hidt, scaled, hg3, hgt, wg, normed_s, unit_s, inv_s, prob_s, rank_s,
    ssend, srecv, part, rsbuf, agbuf,
    in_sem, tok_send, tok_recv, meta_send, meta_recv, row_send, row_recv, sc_send, sc_recv, rs_send, rs_recv, ag_send, ag_recv, hg_sem, wg_sem,
):
    n = n_ep * n_dp
    width, tokens = res_ref.shape
    experts = rwt_ref.shape[0]
    ff = w.shape[0]
    pad_width = send.shape[2]
    plane = n // lines
    group = plane * cap
    me = lax.axis_index("ep") * n_dp + lax.axis_index("dp")
    z = me // plane
    p = me % plane

    def remote(src, dst, s_sem, r_sem, dev_ep, dev_dp):
        return pltpu.make_async_remote_copy(
            src_ref=src, dst_ref=dst, send_sem=s_sem, recv_sem=r_sem,
            device_id=(dev_ep, dev_dp), device_id_type=pl.DeviceIdType.MESH,
        )

    barrier = pltpu.get_barrier_semaphore()

    def greet(i, _):
        @pl.when(i != me)
        def _():
            pl.semaphore_signal(
                barrier, inc=1, device_id=(i // n_dp, i % n_dp), device_id_type=pl.DeviceIdType.MESH
            )
        return 0

    lax.fori_loop(0, n, greet, 0)
    load_h = pltpu.make_async_copy(hidt_any, hidt, in_sem.at[0])
    load_w = pltpu.make_async_copy(w_any, w, in_sem.at[1])
    load_h.start()
    load_w.start()

    gain = jnp.broadcast_to(gain_ref[...], (tokens, width)).T
    ssend[...] = jnp.zeros_like(ssend)
    floated = res_ref[...].astype(F32)
    inverse = lax.rsqrt(jnp.mean(floated * floated, 0, keepdims=True) + 1e-05)
    unit = floated * inverse
    normed = (unit * gain).astype(BF16)
    unit_s[...] = unit
    inv_s[...] = inverse
    normed_s[...] = normed
    logits = jnp.dot(rwt_ref[...], normed, preferred_element_type=F32)
    row_e = lax.broadcasted_iota(jnp.int32, (experts, tokens), 0)
    match = jnp.zeros((experts, tokens), F32)
    ids = ids_ref[...]
    for k in range(ids.shape[0]):
        match = match + jnp.where(ids[k : k + 1, :] == row_e, F32(1.0), F32(0.0))
    expo = jnp.where(match > 0, jnp.exp(logits), F32(0.0))
    prob = expo / jnp.sum(expo, 0, keepdims=True)
    row_t = lax.broadcasted_iota(jnp.int32, (tokens, tokens), 0)
    col_t = lax.broadcasted_iota(jnp.int32, (tokens, tokens), 1)
    before = jnp.where(row_t < col_t, F32(1.0), F32(0.0)).astype(BF16)
    rank = jnp.dot(match.astype(BF16), before, preferred_element_type=F32)
    rank = jnp.where(match > 0, rank, F32(-1.0))
    prob_s[...] = prob
    rank_s[...] = rank
    tok[z] = og_ref[...]
    meta[z] = jnp.concatenate([rank, prob], 0).astype(BF16)

    pl.semaphore_wait(barrier, n - 1)

    def along(src, source, side):
        to = (z + 2 * side - 1) * plane + p
        return (
            remote(src, tok.at[source], tok_send.at[source, side], tok_recv.at[source], to // n_dp, to % n_dp),
            remote(
                meta.at[source], meta.at[source], meta_send.at[source, side], meta_recv.at[source],
                to // n_dp, to % n_dp,
            ),
        )

    def start_along(src, source, side):
        nxt = z + 2 * side - 1

        @pl.when((nxt >= 0) & (nxt < lines))
        def _():
            for c in along(src, source, side):
                c.start()

    start_along(og_ref, z, 0)
    start_along(og_ref, z, 1)

    def sides(k, fn):
        def step(i, _):
            source = z + k * (2 * i - 1)

            @pl.when((source >= 0) & (source < lines) & (k + 1 - i > 0) & (k >= 0))
            def _():
                fn(source, i)
            return 0
        lax.fori_loop(0, 2, step, 0)

    def forward(source, i):
        for c in along(tok.at[source], source, i):
            c.wait_recv()
        start_along(tok.at[source], source, 1 - i)

    def pack(source, _):
        metat[...] = meta[source].astype(F32).reshape(2 * experts, 1, tokens)
        rt = metat[pl.ds(z * plane, plane)]
        pt = metat[pl.ds(experts + z * plane, plane)]
        slot = lax.broadcasted_iota(jnp.int32, (plane, cap, tokens), 1).astype(F32)
        hit = slot == rt
        hot = jnp.where(hit, F32(1.0), F32(0.0)).reshape(group, tokens).astype(BF16)
        weight = jnp.sum(jnp.where(hit, pt, F32(0.0)), -1, keepdims=True)
        rows = lax.dot_general(
            hot, tok[source], (((1,), (1,)), ((), ())), preferred_element_type=F32
        )
        first = source * plane
        send[pl.ds(first, plane), :, pl.ds(0, width)] = rows.reshape(plane, cap, width).astype(BF16)
        send[pl.ds(first, plane), :, pl.ds(width, pad_width - width)] = jnp.broadcast_to(
            weight, (plane, cap, pad_width - width)
        ).astype(BF16)
        own = first + p
        recv[own] = send[own]

        def push(k, _):
            q = (p + k) % plane
            row_copy(first, z * plane + q, q).start()
            return 0

        lax.fori_loop(1, plane, push, 0)

    def row_copy(first, to, q):
        return remote(
            send.at[first + q], recv.at[first + p], row_send.at[first + q], row_recv.at[first + p],
            to // n_dp, to % n_dp,
        )

    def wait_row(first, q):
        to = z * plane + q
        return remote(
            send.at[first + q], recv.at[first + q], row_send.at[first + q], row_recv.at[first + q],
            to // n_dp, to % n_dp,
        )

    def chunk(source, _):
        first = source * plane

        def arrive(k, _):
            wait_row(first, (p + k) % plane).wait_recv()
            return 0

        lax.fori_loop(1, plane, arrive, 0)
        rows = recv[pl.ds(first, plane)].astype(F32).reshape(group, pad_width)
        at = pl.ds(pl.multiple_of(first * cap, group), group)
        h = hid3[source].astype(F32)
        grad = rows[:, :width]
        weight = rows[:, width : width + 1]
        inner = lax.dot_general(
            w[...], grad.astype(BF16), (((1,), (1,)), ((), ())), preferred_element_type=F32
        )
        score = jnp.sum(inner * h, 0, keepdims=True)
        for k in range(plane):
            ssend[first + k, :, pl.ds(0, cap)] = score[:, k * cap : (k + 1) * cap]

        def push(k, _):
            d = first + k

            @pl.when(d != me)
            def _():
                remote(
                    ssend.at[d], srecv.at[me], sc_send.at[d], sc_recv.at[me], d // n_dp, d % n_dp
                ).start()
            return 0

        lax.fori_loop(0, plane, push, 0)

        @pl.when(source == z)
        def _():
            srecv[me] = ssend[me]

        across = jnp.broadcast_to(weight, (group, 128)).T[0:1, :]
        hg3[source] = (across * inner).astype(BF16)
        scaled[at] = (weight * grad).astype(BF16)

    def stage(k, _):
        @pl.when((k > 0) & (k < lines))
        def _():
            sides(k, forward)

        @pl.when(k < lines)
        def _():
            sides(k, pack)

        @pl.when(k == 0)
        def _():
            load_h.wait()
            for i in range(lines):
                hid3[i] = hidt[:, i * group : (i + 1) * group]
            load_w.wait()

        sides(k - 1, chunk)
        return 0

    lax.fori_loop(0, lines + 1, stage, 0)

    for i in range(lines):
        hgt[:, i * group : (i + 1) * group] = hg3[i]
    store_h = pltpu.make_async_copy(hgt, hgt_any, hg_sem)
    store_h.start()

    blocks = wg_sem.shape[0]
    rows_of = ff // blocks

    def wg_copy(b):
        at = pl.ds(pl.multiple_of(b * rows_of, rows_of), rows_of)
        return pltpu.make_async_copy(wg.at[b % 2], wg_any.at[at], wg_sem.at[b])

    def wg_block(b, _):
        @pl.when(b >= 2)
        def _():
            wg_copy(b - 2).wait()

        at = pl.ds(pl.multiple_of(b * rows_of, rows_of), rows_of)
        wg[b % 2] = jnp.dot(hidt[at], scaled[...], preferred_element_type=F32).astype(BF16)
        wg_copy(b).start()
        return 0

    def others(fn):
        def step(i, _):
            @pl.when(i != me)
            def _():
                fn(i)
            return 0
        lax.fori_loop(0, n, step, 0)

    cut1, cut2 = blocks // 5, (3 * blocks) // 5
    lax.fori_loop(0, cut1, wg_block, 0)

    others(lambda i: remote(ssend.at[i], srecv.at[i], sc_send.at[i], sc_recv.at[i], i // n_dp, i % n_dp).wait_recv())
    back = srecv[...].reshape(n, 128)
    rank = rank_s[...]
    prob = prob_s[...]
    score = jnp.zeros((experts, tokens), F32)
    for r in range(cap):
        score = score + jnp.where(rank == F32(r), back[:, r : r + 1], F32(0.0))
    lg = prob * (score - jnp.sum(prob * score, 0, keepdims=True))
    hi = lg.astype(BF16)
    lo = (lg - hi.astype(F32)).astype(BF16)
    both = lax.dot_general(
        jnp.concatenate([hi, lo], 0), normed_s[...], (((1,), (1,)), ((), ())),
        preferred_element_type=F32,
    )
    router = both[:experts] + both[experts:]
    for e in range(experts):
        part[e] = router[e : e + 1, :]
    rsbuf[me] = part[me]
    others(lambda i: remote(part.at[i], rsbuf.at[me], rs_send.at[i], rs_recv.at[me], i // n_dp, i % n_dp).start())

    lax.fori_loop(cut1, cut2, wg_block, 0)

    others(lambda i: remote(part.at[i], rsbuf.at[i], rs_send.at[i], rs_recv.at[i], i // n_dp, i % n_dp).wait_recv())
    agbuf[me] = jnp.sum(rsbuf[...], 0)
    others(lambda i: remote(agbuf.at[me], agbuf.at[me], ag_send.at[i], ag_recv.at[me], i // n_dp, i % n_dp).start())

    rwt = rwt_ref[...]
    ngrad = lax.dot_general(
        jnp.concatenate([rwt, rwt], 0), jnp.concatenate([hi, lo], 0), (((0,), (0,)), ((), ())),
        preferred_element_type=F32,
    )
    upper = ngrad * jnp.broadcast_to(gain_ref[...], (tokens, width)).T
    unit = unit_s[...]
    mean = jnp.mean(upper * unit, 0, keepdims=True)
    rg_ref[...] = (inv_s[...] * (upper - unit * mean)).astype(BF16)

    lax.fori_loop(cut2, blocks, wg_block, 0)

    others(lambda i: remote(agbuf.at[me], agbuf.at[i], ag_send.at[i], ag_recv.at[i], i // n_dp, i % n_dp).wait_recv())
    total = agbuf[...].reshape(experts, width)
    rgt_ref[...] = total
    gg_ref[...] = jnp.sum(total * rwt.astype(F32), 0, keepdims=True) / gain_ref[...]

    def finish(i):
        remote(ssend.at[i], srecv.at[me], sc_send.at[i], sc_recv.at[me], i // n_dp, i % n_dp).wait_send()
        remote(part.at[i], rsbuf.at[me], rs_send.at[i], rs_recv.at[me], i // n_dp, i % n_dp).wait_send()
        remote(agbuf.at[me], agbuf.at[me], ag_send.at[i], ag_recv.at[me], i // n_dp, i % n_dp).wait_send()

    others(finish)

    def finish_rows(source, _):
        def step(k, _):
            q = (p + k) % plane
            row_copy(source * plane, z * plane + q, q).wait_send()
            return 0
        lax.fori_loop(1, plane, step, 0)

        def sent(side):
            nxt = z + 2 * side - 1

            @pl.when((nxt >= 0) & (nxt < lines))
            def _():
                for c in along(tok.at[source], source, side):
                    c.wait_send()

        @pl.when(source <= z)
        def _():
            sent(1)

        @pl.when(source >= z)
        def _():
            sent(0)
        return 0

    lax.fori_loop(0, lines, finish_rows, 0)

    store_h.wait()
    for b in range(max(0, blocks - 2), blocks):
        wg_copy(b).wait()


def on_device(n_ep, n_dp, residual, norm_gain, router_weight, out_grad, expert_ids, hidden, down_weight):
    n = n_ep * n_dp
    lines = math.gcd(n_ep, LINE)
    tokens, width = residual.shape
    experts = router_weight.shape[1]
    slots, ff = hidden.shape[1:]
    real_cap = slots // experts
    cap = -(-real_cap // 8) * 8
    pad_width = -(-(width + 1) // 128) * 128
    hidt = hidden[0].T
    if cap != real_cap:
        hidt = jnp.pad(
            hidt.reshape(ff, experts, real_cap), ((0, 0), (0, 0), (0, cap - real_cap))
        ).reshape(ff, experts * cap)
    rows = experts * cap
    blocks = max(b for b in range(1, 6) if ff % (b * 16) == 0)
    vmem = pl.BlockSpec(memory_space=pltpu.VMEM)
    anyspace = pl.BlockSpec(memory_space=pl.ANY)
    dma = pltpu.SemaphoreType.DMA
    hgt, wg, rg, rgt, gg = pl.pallas_call(
        functools.partial(kernel, n_ep, n_dp, lines, cap),
        out_shape=(
            jax.ShapeDtypeStruct((ff, rows), BF16),
            jax.ShapeDtypeStruct((ff, width), BF16),
            jax.ShapeDtypeStruct((width, tokens), BF16),
            jax.ShapeDtypeStruct((experts, width), F32),
            jax.ShapeDtypeStruct((1, width), F32),
        ),
        in_specs=[vmem] * 5 + [anyspace] * 2,
        out_specs=(anyspace, anyspace, vmem, vmem, vmem),
        scratch_shapes=[
            pltpu.VMEM((lines, width, tokens), BF16),
            pltpu.VMEM((lines, 2 * experts, tokens), BF16),
            pltpu.VMEM((2 * experts, 1, tokens), F32),
            pltpu.VMEM((n, cap, pad_width), BF16),
            pltpu.VMEM((n, cap, pad_width), BF16),
            pltpu.VMEM((ff, width), BF16),
            pltpu.VMEM((lines, ff, rows // lines), BF16),
            pltpu.VMEM((ff, rows), BF16),
            pltpu.VMEM((rows, width), BF16),
            pltpu.VMEM((lines, ff, rows // lines), BF16),
            pltpu.VMEM((ff, rows), BF16),
            pltpu.VMEM((2, ff // blocks, width), BF16),
            pltpu.VMEM((width, tokens), BF16),
            pltpu.VMEM((width, tokens), F32),
            pltpu.VMEM((1, tokens), F32),
            pltpu.VMEM((experts, tokens), F32),
            pltpu.VMEM((experts, tokens), F32),
            pltpu.VMEM((n, 1, 128), F32),
            pltpu.VMEM((n, 1, 128), F32),
            pltpu.VMEM((n, 1, width), F32),
            pltpu.VMEM((n, 1, width), F32),
            pltpu.VMEM((n, 1, width), F32),
            dma((2,)),
            dma((lines, 2)), dma((lines,)), dma((lines, 2)), dma((lines,)),
            dma((n,)), dma((n,)), dma((n,)), dma((n,)),
            dma((n,)), dma((n,)), dma((n,)), dma((n,)),
            dma,
            dma((blocks,)),
        ],
        compiler_params=pltpu.CompilerParams(
            collective_id=0, has_side_effects=True, vmem_limit_bytes=67_000_000
        ),
        name="expert_backward",
    )(residual.T, norm_gain[None], router_weight.T, out_grad.T, expert_ids.T, hidt, down_weight[0])
    if cap != real_cap:
        hgt = hgt.reshape(ff, experts, cap)[:, :, :real_cap].reshape(ff, slots)
    return hgt.T[None], wg[None], rg.T, rgt.T, gg[0]


def solution(mesh):
    both = ("ep", "dp")
    return jax.shard_map(
        functools.partial(on_device, mesh.shape["ep"], mesh.shape["dp"]),
        mesh=mesh,
        in_specs=(P(both, None), P(), P(), P(both, None), P(both, None), P(both, None, None), P(both, None, None)),
        out_specs=(P(both, None, None), P(both, None, None), P(both, None), P(), P()),
        check_vma=False,
    )
```

profile of v0, /device:TPU:0, one launch (start us, length us, event | category | flops | bytes accessed | tf_op | source)
XLA Modules:
  0.0 119.1 jit_solution(13313513826478395642)
XLA Ops:
  0.6 1.3 %broadcast_in_dim.9.gain_ref = f32[1,2880]{1,0:T(1,128)} reshape(f32[2880]{0:T(1024)} %param.8) | data formatting | bytes 23040 | tf_op jit(solution)/shard_map/broadcast_in_dim | solution.py:400
  1.9 103.6 %expert_backward.1 = (bf16[1440,768]{1,0:T(8,128)(2,1)}, bf16[1440,2880]{1,0:T(8,128)(2,1)}, bf16[2880,128]{1,0:T(8,128)(2,1)}, f32[32,2880]{1,0:T(8,128)}, f32[1,2880]{1,0:T(1,128)}) custom-call(bf16[2880,128]{1,0:T(8,128)(2,1)} %bitcast.19, f32[1,2880]{1,0:T(1,128)} %broadcast_in_dim.9.gain_ref, bf16[32,2880]{1,0:T(8,128)(2,1)} %bitcast.22, ...), custom_call_target="tpu_custom_call" | custom-call | tf_op jit(solution)/shard_map/expert_backward/pallas_call | solution.py:355
  105.5 1.3 %reduce = f32[2880]{0:T(1024)} reduce(f32[1,2880]{1,0:T(1,128)} %get-tuple-element.14, f32[]{:T(128)} %constant.2), dimensions={0}, to_apply=%get-tuple-element.14.reduce_sub_computation | reduce | bytes 23044 | tf_op jit(solution)/shard_map/expert_backward/pallas_call | solution.py:355
  106.9 3.1 %copy.16 = bf16[1,768,1440]{1,2,0:T(8,128)(2,1)} copy(bf16[1,768,1440]{1,2,0:T(8,128)(2,1)} %bitcast.17) | data formatting | bytes 4423680
  110.0 0.0 copy-start
  110.0 0.0 copy-start.1
  110.0 7.5 %copy.17 = bf16[1,1440,2880]{2,1,0:T(8,128)(2,1)} copy(bf16[1,1440,2880]{2,1,0:T(8,128)(2,1)} %bitcast.15) | data formatting | bytes 16588800
  117.5 0.0 copy-done
  117.5 0.9 copy.18
  118.4 0.0 copy-done.1
  118.4 0.7 copy.19
Async XLA Ops:
  110.0 7.5 %copy-start = (bf16[2880,128]{1,0:T(8,128)(2,1)S(1)}, bf16[2880,128]{1,0:T(8,128)(2,1)}, u32[]{:S(2)}) copy-start(bf16[2880,128]{1,0:T(8,128)(2,1)} %get-tuple-element.12) | copy-start | bytes 2211844
  110.0 8.4 %copy-start.1 = (f32[32,2880]{1,0:T(8,128)S(1)}, f32[32,2880]{1,0:T(8,128)}, u32[]{:S(2)}) copy-start(f32[32,2880]{1,0:T(8,128)} %get-tuple-element.13) | copy-start | bytes 1105924
where the time goes:
time: 120 us; the launch traced here: 119 us
  Pallas kernels  104 us (87%)
  local copies, waits for them, and re-layouts  13.6 us (11%)
  other arithmetic  1.34 us (1%)
    pallas_call x1, Pallas kernels, on_device(): pl.pallas_call(functools.partial(kernel, n_ep, n_dp, lines, cap), out_sha...  104 us
    unnamed x8, local copies, waits for them, and re-layouts  12.2 us

commit v1 on v0

v1 whole, which is shorter than its diff:
```python
import functools
import math

import jax
import jax.numpy as jnp
from jax import lax
from jax.experimental import pallas as pl
from jax.experimental.pallas import tpu as pltpu
from jax.sharding import PartitionSpec as P

F32 = jnp.float32
BF16 = jnp.bfloat16
LINE = 4
PIECES = 3


def kernel(
    n_ep, n_dp, lines, cap, cuts,
    res_any, gain_any, rwt_any, og_any, ids_any, hidt_any, w_any,
    hgt, wg, rg_ref, rgt_ref, gg_ref,
    res_s, gain_s, rwt_s, ids_s, tok, meta, metat, hot_s, send, recv, w, hid3, hidt, inner_s, scaled, normed_s, inv_s,
    prob_s, rank_s, ssend, srecv, part, rsbuf, agbuf,
    in_sem, tok_send, tok_recv, meta_send, meta_recv, row_send, row_recv, sc_send, sc_recv, rs_send, rs_recv, ag_send, ag_recv,
):
    n = n_ep * n_dp
    width, tokens = res_s.shape
    experts = rwt_s.shape[0]
    ff = w.shape[0]
    pad_width = send.shape[2]
    plane = n // lines
    group = plane * cap
    pieces = len(cuts)
    owned = part.shape[0]
    me = lax.axis_index("ep") * n_dp + lax.axis_index("dp")
    mine = (me * owned + n - 1) // n
    owner = mine * n < (me + 1) * owned
    z = me // plane
    p = me % plane

    def remote(src, dst, s_sem, r_sem, dev_ep, dev_dp):
        return pltpu.make_async_remote_copy(
            src_ref=src, dst_ref=dst, send_sem=s_sem, recv_sem=r_sem,
            device_id=(dev_ep, dev_dp), device_id_type=pl.DeviceIdType.MESH,
        )

    barrier = pltpu.get_barrier_semaphore()

    def hello(to):
        pl.semaphore_signal(
            barrier, inc=1, device_id=(to // n_dp, to % n_dp), device_id_type=pl.DeviceIdType.MESH
        )

    for side in range(2):
        nxt = z + 2 * side - 1

        @pl.when((nxt >= 0) & (nxt < lines))
        def _():
            hello(nxt * plane + p)

    def greet(k, _):
        hello(z * plane + (p + k) % plane)
        return 0

    lax.fori_loop(1, plane, greet, 0)

    load_og = pltpu.make_async_copy(og_any, tok.at[z], in_sem.at[0])
    loads = [
        pltpu.make_async_copy(res_any, res_s, in_sem.at[1]),
        pltpu.make_async_copy(gain_any, gain_s, in_sem.at[2]),
        pltpu.make_async_copy(rwt_any, rwt_s, in_sem.at[3]),
        pltpu.make_async_copy(ids_any, ids_s, in_sem.at[4]),
    ]
    load_h = pltpu.make_async_copy(hidt_any, hidt, in_sem.at[5])
    load_w = pltpu.make_async_copy(w_any, w, in_sem.at[6])
    load_og.start()
    for c in loads:
        c.start()
    load_h.start()
    load_w.start()

    def tok_copy(source, side, j):
        to = (z + 2 * side - 1) * plane + p
        at = pl.ds(cuts[j][0], cuts[j][1])
        return remote(
            tok.at[source, at], tok.at[source, at], tok_send.at[source, side], tok_recv.at[source, j],
            to // n_dp, to % n_dp,
        )

    def meta_copy(source, side):
        to = (z + 2 * side - 1) * plane + p
        return remote(
            meta.at[source], meta.at[source], meta_send.at[source, side], meta_recv.at[source],
            to // n_dp, to % n_dp,
        )

    def along(source, side, j):
        return [tok_copy(source, side, j)] + ([meta_copy(source, side)] if j == 0 else [])

    def to_side(side, copies):
        nxt = z + 2 * side - 1

        @pl.when((nxt >= 0) & (nxt < lines))
        def _():
            for c in copies:
                c.start()

    ssend[...] = jnp.zeros_like(ssend)
    part[owned - 1] = jnp.zeros(part.shape[1:], BF16)
    load_og.wait()
    neighbours = jnp.where(z > 0, 1, 0) + jnp.where(z < lines - 1, 1, 0)
    pl.semaphore_wait(barrier, plane - 1 + neighbours)
    for side in range(2):
        to_side(side, [tok_copy(z, side, 0)])

    for c in loads:
        c.wait()
    gain_row = gain_s[...].reshape(1, width)
    gain = jnp.broadcast_to(gain_row, (tokens, width)).T
    floated = res_s[...].astype(F32)
    inverse = lax.rsqrt(jnp.mean(floated * floated, 0, keepdims=True) + 1e-05)
    unit = floated * inverse
    normed = (unit * gain).astype(BF16)
    inv_s[...] = inverse
    normed_s[...] = normed
    logits = jnp.dot(rwt_s[...], normed, preferred_element_type=F32)
    row_e = lax.broadcasted_iota(jnp.int32, (experts, tokens), 0)
    match = jnp.zeros((experts, tokens), F32)
    ids = ids_s[...]
    for k in range(ids.shape[0]):
        match = match + jnp.where(ids[k : k + 1, :] == row_e, F32(1.0), F32(0.0))
    expo = jnp.where(match > 0, jnp.exp(logits), F32(0.0))
    prob = expo / jnp.sum(expo, 0, keepdims=True)
    row_t = lax.broadcasted_iota(jnp.int32, (tokens, tokens), 0)
    col_t = lax.broadcasted_iota(jnp.int32, (tokens, tokens), 1)
    before = jnp.where(row_t < col_t, F32(1.0), F32(0.0)).astype(BF16)
    rank = jnp.dot(match.astype(BF16), before, preferred_element_type=F32)
    rank = jnp.where(match > 0, rank, F32(-1.0))
    prob_s[...] = prob
    rank_s[...] = rank
    meta[z] = jnp.concatenate([rank, prob], 0).astype(BF16)

    for side in range(2):
        to_side(side, [meta_copy(z, side)])
    for j in range(1, pieces):
        for side in range(2):
            to_side(side, [tok_copy(z, side, j)])

    def sides(k, fn):
        def step(i, _):
            source = z + k * (2 * i - 1)

            @pl.when((source >= 0) & (source < lines) & (k + 1 - i > 0) & (k >= 0))
            def _():
                fn(source, i)
            return 0
        lax.fori_loop(0, 2, step, 0)

    def onward(i):
        nxt = z + 1 - 2 * i
        return (nxt >= 0) & (nxt < lines)

    def relay(j, source, i):
        @pl.when(onward(i))
        def _():
            for c in along(source, i, j):
                c.wait_recv()
            for c in along(source, 1 - i, j):
                c.start()

    def settle(j, source, i):
        @pl.when(jnp.logical_not(onward(i)))
        def _():
            for c in along(source, i, j):
                c.wait_recv()

    def cols(j):
        return cuts[j][0], cuts[j][1] + (pad_width - width if j == 0 else 0)

    def pack(j, source, i):
        first = source * plane
        lane0, lanes = cuts[j]
        if j == 0:
            metat[...] = meta[source].astype(F32).reshape(2 * experts, 1, tokens)
            rt = metat[pl.ds(z * plane, plane)]
            pt = metat[pl.ds(experts + z * plane, plane)]
            slot = lax.broadcasted_iota(jnp.int32, (plane, cap, tokens), 1).astype(F32)
            hit = slot == rt
            hot = jnp.where(hit, F32(1.0), F32(0.0)).reshape(group, tokens).astype(BF16)
            weight = jnp.sum(jnp.where(hit, pt, F32(0.0)), -1, keepdims=True)
            hot_s[i] = hot
            send[pl.ds(first, plane), :, pl.ds(width, pad_width - width)] = jnp.broadcast_to(
                weight, (plane, cap, pad_width - width)
            ).astype(BF16)
        else:
            hot = hot_s[i]
        rows = lax.dot_general(
            hot, tok[source, pl.ds(lane0, lanes)], (((1,), (1,)), ((), ())), preferred_element_type=F32
        )
        send[pl.ds(first, plane), :, pl.ds(lane0, lanes)] = rows.reshape(plane, cap, lanes).astype(BF16)
        own = first + p
        at = pl.ds(*cols(j))
        recv[own, :, at] = send[own, :, at]

        def push(k, _):
            row_copy(source, (p + k) % plane, p, j).start()
            return 0

        lax.fori_loop(1, plane, push, 0)

    def row_copy(source, q, slot, j):
        first = source * plane
        to = z * plane + q
        at = pl.ds(*cols(j))
        return remote(
            send.at[first + q, :, at], recv.at[first + slot, :, at], row_send.at[0], row_recv.at[source, j],
            to // n_dp, to % n_dp,
        )

    def all_of(ref, s_sem, r_sem):
        return remote(ref, ref, s_sem, r_sem, 0, 0)

    def chunk(j, source, i):
        first = source * plane
        lane0, lanes = cuts[j]

        landed = recv.at[pl.ds(first, plane - 1), :, pl.ds(*cols(j))]
        all_of(landed, row_send.at[0], row_recv.at[source, j]).wait_recv()
        at = pl.ds(pl.multiple_of(first * cap, group), group)
        tail = recv[pl.ds(first, plane), :, pl.ds(pad_width - 128, 128)].astype(F32).reshape(group, 128)
        weight = tail[:, width - pad_width + 128 : width - pad_width + 129]
        grad = recv[pl.ds(first, plane), :, pl.ds(lane0, lanes)].astype(F32).reshape(group, lanes)
        inner = lax.dot_general(
            w[:, lane0 : lane0 + lanes], grad.astype(BF16), (((1,), (1,)), ((), ())), preferred_element_type=F32
        )
        if j > 0:
            inner = inner_s[i] + inner
        if j < pieces - 1:
            inner_s[i] = inner
        else:
            score = jnp.sum(inner * hid3[source].astype(F32), 0, keepdims=True)
            for k in range(plane):
                ssend[first + k, :, pl.ds(0, cap)] = score[:, k * cap : (k + 1) * cap]

            def push(k, _):
                d = first + k

                @pl.when(d != me)
                def _():
                    remote(
                        ssend.at[d], srecv.at[me], sc_send.at[0], sc_recv.at[0], d // n_dp, d % n_dp
                    ).start()
                return 0

            lax.fori_loop(0, plane, push, 0)

            @pl.when(source == z)
            def _():
                srecv[me] = ssend[me]

            across = jnp.broadcast_to(weight, (group, 128)).T[0:1, :]
            grad_h = (across * inner).astype(BF16)
            for b in range(lines):
                @pl.when(source == b)
                def _(b=b):
                    hgt[:, b * group : (b + 1) * group] = grad_h
        scaled[at, lane0 : lane0 + lanes] = (weight * grad).astype(BF16)

    def stage(k, _):
        for j in range(pieces):
            @pl.when((k > 0) & (k < lines))
            def _(j=j):
                sides(k, functools.partial(settle, j))

            @pl.when(k < lines)
            def _(j=j):
                sides(k, functools.partial(pack, j))

            later = k + (j + 1) // pieces

            @pl.when((later > 0) & (later < lines))
            def _(j=j, later=later):
                sides(later, functools.partial(relay, (j + 1) % pieces))

            if j == min(1, pieces - 1):
                @pl.when(k == 0)
                def _():
                    load_h.wait()
                    for i in range(lines):
                        hid3[i] = hidt[:, i * group : (i + 1) * group]
                    load_w.wait()

            if j > 0:
                sides(k, functools.partial(chunk, j - 1))
            else:
                sides(k - 1, functools.partial(chunk, pieces - 1))
        return 0

    lax.fori_loop(0, lines + 1, stage, 0)

    blocks = max(b for b in range(1, 6) if ff % (b * 16) == 0)
    rows_of = ff // blocks

    def wg_block(b, _):
        at = pl.ds(pl.multiple_of(b * rows_of, rows_of), rows_of)
        wg[at] = jnp.dot(hidt[at], scaled[...], preferred_element_type=F32).astype(BF16)
        return 0

    def others(fn):
        def step(i, _):
            @pl.when(i != me)
            def _():
                fn(i)
            return 0
        lax.fori_loop(0, n, step, 0)

    cut1, cut2 = (2 * blocks) // 5, (4 * blocks) // 5
    lax.fori_loop(0, cut1, wg_block, 0)

    all_of(srecv.at[pl.ds(0, n - 1)], sc_send.at[0], sc_recv.at[0]).wait_recv()
    back = srecv[...].reshape(n, 128)
    rank = rank_s[...]
    prob = prob_s[...]
    score = jnp.zeros((experts, tokens), F32)
    for r in range(cap):
        score = score + jnp.where(rank == F32(r), back[:, r : r + 1], F32(0.0))
    lg = prob * (score - jnp.sum(prob * score, 0, keepdims=True))
    hi = lg.astype(BF16)
    lo = (lg - hi.astype(F32)).astype(BF16)
    both = lax.dot_general(
        jnp.concatenate([hi, lo], 0), normed_s[...], (((1,), (1,)), ((), ())),
        preferred_element_type=F32,
    )
    router = (both[:experts] + both[experts:]).astype(BF16)
    for b in range(owned):
        lanes = min(128, width - b * 128)
        part[b, :, pl.ds(0, lanes)] = router[:, b * 128 : b * 128 + lanes]

    def share(b, _):
        to = b * n // owned

        @pl.when(to != me)
        def _():
            remote(part.at[b], rsbuf.at[me], rs_send.at[0], rs_recv.at[0], to // n_dp, to % n_dp).start()
        return 0

    lax.fori_loop(0, owned, share, 0)

    @pl.when(owner)
    def _():
        rsbuf[me] = part[mine]

    lax.fori_loop(cut1, cut2, wg_block, 0)

    @pl.when(owner)
    def _():
        all_of(rsbuf.at[pl.ds(0, n - 1)], rs_send.at[0], rs_recv.at[0]).wait_recv()
        agbuf[mine] = jnp.sum(rsbuf[...].astype(F32), 0).astype(BF16)
        others(lambda i: remote(agbuf.at[mine], agbuf.at[mine], ag_send.at[0], ag_recv.at[0], i // n_dp, i % n_dp).start())

    rwt = rwt_s[...]
    ngrad = lax.dot_general(
        jnp.concatenate([rwt, rwt], 0), jnp.concatenate([hi, lo], 0), (((0,), (0,)), ((), ())),
        preferred_element_type=F32,
    )
    upper = ngrad * jnp.broadcast_to(gain_s[...].reshape(1, width), (tokens, width)).T
    unit = res_s[...].astype(F32) * inv_s[...]
    mean = jnp.mean(upper * unit, 0, keepdims=True)
    rg_ref[...] = (inv_s[...] * (upper - unit * mean)).astype(BF16)

    lax.fori_loop(cut2, blocks, wg_block, 0)

    all_of(send.at[pl.ds(0, lines * (plane - 1))], row_send.at[0], row_recv.at[0, 0]).wait_send()

    def finish_toks(source, _):
        def sent(side):
            nxt = z + 2 * side - 1

            @pl.when((nxt >= 0) & (nxt < lines))
            def _():
                all_of(tok.at[source], tok_send.at[source, side], tok_recv.at[source, 0]).wait_send()
                meta_copy(source, side).wait_send()

        @pl.when(source <= z)
        def _():
            sent(1)

        @pl.when(source >= z)
        def _():
            sent(0)
        return 0

    lax.fori_loop(0, lines, finish_toks, 0)
    all_of(ssend.at[pl.ds(0, n - 1)], sc_send.at[0], sc_recv.at[0]).wait_send()

    @pl.when(owner)
    def _():
        all_of(part.at[pl.ds(0, owned - 1)], rs_send.at[0], rs_recv.at[0]).wait_send()
        all_of(agbuf.at[pl.ds(0, owned - 1)], ag_send.at[0], ag_recv.at[0]).wait_recv()

    @pl.when(jnp.logical_not(owner))
    def _():
        all_of(part.at[pl.ds(0, owned)], rs_send.at[0], rs_recv.at[0]).wait_send()
        all_of(agbuf.at[pl.ds(0, owned)], ag_send.at[0], ag_recv.at[0]).wait_recv()

    gain_row = gain_s[...].reshape(1, width)
    for b in range(owned):
        lanes = min(128, width - b * 128)
        at = slice(b * 128, b * 128 + lanes)
        total = agbuf[b, :, pl.ds(0, lanes)].astype(F32)
        rgt_ref[:, at] = total
        gg_ref[:, at] = jnp.sum(total * rwt_s[:, at].astype(F32), 0, keepdims=True) / gain_row[:, at]


    @pl.when(owner)
    def _():
        all_of(rsbuf.at[pl.ds(0, n - 1)], ag_send.at[0], ag_recv.at[0]).wait_send()


def store(hgt, wg, rg, rgt, gg, hgt_any, wg_any, rg_any, rgt_any, gg_any, sem):
    ff = wg.shape[0]
    blocks = max(b for b in range(1, 7) if ff % (b * 16) == 0)
    rows = ff // blocks
    copies = [
        pltpu.make_async_copy(wg.at[pl.ds(b * rows, rows)], wg_any.at[pl.ds(b * rows, rows)], sem.at[4 + b])
        for b in range(blocks)
    ]
    copies += [
        pltpu.make_async_copy(hgt, hgt_any, sem.at[0]),
        pltpu.make_async_copy(rg, rg_any, sem.at[1]),
        pltpu.make_async_copy(rgt, rgt_any, sem.at[2]),
        pltpu.make_async_copy(gg.at[0], gg_any, sem.at[3]),
    ]
    for c in copies:
        c.start()
    for c in copies:
        c.wait()


def column_cuts(width, pad_width, count):
    tiles = pad_width // 128
    sizes = [tiles // count + (1 if i < tiles % count else 0) for i in range(count)]
    last = (tiles - sizes[0]) * 128
    cuts = [(last, width - last)]
    at = 0
    for s in sizes[1:]:
        cuts.append((at, s * 128))
        at += s * 128
    return tuple(cuts)


def on_device(n_ep, n_dp, residual, norm_gain, router_weight, out_grad, expert_ids, hidden, down_weight):
    n = n_ep * n_dp
    lines = math.gcd(n_ep, LINE)
    tokens, width = residual.shape
    topk = expert_ids.shape[1]
    experts = router_weight.shape[1]
    slots, ff = hidden.shape[1:]
    real_cap = slots // experts
    cap = -(-real_cap // 8) * 8
    pad_width = -(-(width + 1) // 128) * 128
    hidt = hidden[0].T
    if cap != real_cap:
        hidt = jnp.pad(
            hidt.reshape(ff, experts, real_cap), ((0, 0), (0, 0), (0, cap - real_cap))
        ).reshape(ff, experts * cap)
    rows = experts * cap
    plane = n // lines
    group = plane * cap
    owned = -(-width // 128)
    assert owned <= n
    cuts = column_cuts(width, pad_width, PIECES)
    vmem = pl.BlockSpec(memory_space=pltpu.VMEM)
    anyspace = pl.BlockSpec(memory_space=pl.ANY)
    dma = pltpu.SemaphoreType.DMA

    def far(x):
        return pltpu.with_memory_space_constraint(x, pltpu.HBM)

    outs = (((ff, rows), BF16), ((ff, width), BF16), ((width, tokens), BF16), ((experts, width), F32))
    held = pl.pallas_call(
        functools.partial(kernel, n_ep, n_dp, lines, cap, cuts),
        out_shape=tuple(pltpu.VMEM(s, t) for s, t in outs) + (pltpu.VMEM((1, width), F32),),
        in_specs=[anyspace] * 7,
        out_specs=(vmem,) * 5,
        scratch_shapes=[
            pltpu.VMEM((width, tokens), BF16),
            pltpu.VMEM((width,), F32),
            pltpu.VMEM((experts, width), BF16),
            pltpu.VMEM((topk, tokens), jnp.int32),
            pltpu.VMEM((lines, width, tokens), BF16),
            pltpu.VMEM((lines, 2 * experts, tokens), BF16),
            pltpu.VMEM((2 * experts, 1, tokens), F32),
            pltpu.VMEM((2, group, tokens), BF16),
            pltpu.VMEM((n, cap, pad_width), BF16),
            pltpu.VMEM((n, cap, pad_width), BF16),
            pltpu.VMEM((ff, width), BF16),
            pltpu.VMEM((lines, ff, group), BF16),
            pltpu.VMEM((ff, rows), BF16),
            pltpu.VMEM((2, ff, group), F32),
            pltpu.VMEM((rows, width), BF16),
            pltpu.VMEM((width, tokens), BF16),
            pltpu.VMEM((1, tokens), F32),
            pltpu.VMEM((experts, tokens), F32),
            pltpu.VMEM((experts, tokens), F32),
            pltpu.VMEM((n, 1, 128), F32),
            pltpu.VMEM((n, 1, 128), F32),
            pltpu.VMEM((owned, experts, 128), BF16),
            pltpu.VMEM((n, experts, 128), BF16),
            pltpu.VMEM((owned, experts, 128), BF16),
            dma((7,)),
            dma((lines, 2)), dma((lines, PIECES)), dma((lines, 2)), dma((lines,)),
            dma((1,)), dma((lines, PIECES)), dma((1,)), dma((1,)),
            dma((1,)), dma((1,)), dma((1,)), dma((1,)),
        ],
        compiler_params=pltpu.CompilerParams(
            collective_id=0, has_side_effects=True, vmem_limit_bytes=53_000_000
        ),
        name="expert_backward",
    )(*(far(x) for x in (residual.T, norm_gain, router_weight.T, out_grad.T, expert_ids.T, hidt, down_weight[0])))
    hgt, wg, rg, rgt, gg = pl.pallas_call(
        store,
        out_shape=tuple(jax.ShapeDtypeStruct(s, t) for s, t in outs) + (jax.ShapeDtypeStruct((width,), F32),),
        in_specs=[vmem] * 5,
        out_specs=(anyspace,) * 5,
        scratch_shapes=[dma((10,))],
        compiler_params=pltpu.CompilerParams(vmem_limit_bytes=2_000_000),
        name="store",
    )(*held)
    if cap != real_cap:
        hgt = hgt.reshape(ff, experts, cap)[:, :, :real_cap].reshape(ff, slots)
    return hgt.T[None], wg[None], rg.T, rgt.T, gg


def solution(mesh):
    both = ("ep", "dp")
    return jax.shard_map(
        functools.partial(on_device, mesh.shape["ep"], mesh.shape["dp"]),
        mesh=mesh,
        in_specs=(P(both, None), P(), P(), P(both, None), P(both, None), P(both, None, None), P(both, None, None)),
        out_specs=(P(both, None, None), P(both, None, None), P(both, None), P(), P()),
        check_vma=False,
    )
```

time: 120 us -> 84.9 us (0.71)
  Pallas kernels: 104 us -> 84.1 us
  local copies, waits for them, and re-layouts: 13.6 us -> 0 us
  other arithmetic: 1.34 us -> 0 us
    pallas_call x1 -> x2, Pallas kernels: 104 us -> 84.1 us  [the longest x1 79.8 us: on_device(): pl.pallas_call(functools.partial(kernel, n_ep, n_dp, lines, cap, cuts), o...]
    unnamed x8 -> x0, local copies, waits for them, and re-layouts: 12.2 us -> none
    pallas_call x1 -> x0, other arithmetic: 1.34 us -> none  [on_device(): pl.pallas_call(functools.partial(kernel, n_ep, n_dp, lines, cap), out_sha...]
    broadcast_in_dim x1 -> x0, local copies, waits for them, and re-layouts: 1.32 us -> none  [on_device(): norm_gain[None]]
where the time goes in v1:
time: 84.9 us; the launch traced here: 84.8 us
  Pallas kernels  84.1 us (99%)
    pallas_call x1, Pallas kernels, on_device(): pl.pallas_call(functools.partial(kernel, n_ep, n_dp, lines, cap, cuts), o...  79.8 us
    pallas_call x1, Pallas kernels, on_device(): pl.pallas_call(store, out_shape=tuple((jax.ShapeDtypeStruct(s, t) for s,...  4.39 us

profile of v1, /device:TPU:0, one launch (start us, length us, event | category | flops | bytes accessed | tf_op | source)
XLA Modules:
  0.0 84.8 jit_solution(16859523134992743038)
XLA Ops:
  0.6 79.8 %expert_backward.1 = (bf16[1440,768]{1,0:T(8,128)(2,1)S(1)}, bf16[1440,2880]{1,0:T(8,128)(2,1)S(1)}, bf16[2880,128]{1,0:T(8,128)(2,1)S(1)}, f32[32,2880]{1,0:T(8,128)S(1)}, f32[1,2880]{1,0:T(1,128)S(1)}) custom-call(bf16[2880,128]{1,0:T(8,128)(2,1)} %bitcast.16, f32[2880]{0:T(1024)} %gain_any.1, bf16[32,2880]{1,0:T(8,128)(2,1)} %bitcast.18, ...), custom_call_target="tpu_custom_call" | custom-call | tf_op jit(solution)/shard_map/expert_backward/pallas_call | solution.py:480
  80.4 4.4 %store.1 = (bf16[1440,768]{1,0:T(8,128)(2,1)}, bf16[1440,2880]{1,0:T(8,128)(2,1)}, bf16[2880,128]{1,0:T(8,128)(2,1)}, f32[32,2880]{1,0:T(8,128)}, f32[2880]{0:T(1024)}) custom-call(bf16[1440,768]{1,0:T(8,128)(2,1)S(1)} %get-tuple-element.15.hgt, bf16[1440,2880]{1,0:T(8,128)(2,1)S(1)} %get-tuple-element.16.wg, bf16[2880,128]{1,0:T(8,128)(2,1)S(1)} %get-tuple-element.17.rg, ...), custom_call_target="tpu_custom_call" | custom-call | tf_op jit(solution)/shard_map/store/pallas_call | solution.py:520

commit v2 on v1

--- a/solution.py
+++ b/solution.py
@@ -11,29 +11,34 @@
 F32 = jnp.float32
 BF16 = jnp.bfloat16
 LINE = 4
-PIECES = 3
+SHARES = (9, 7, 4, 3)
+PIECES = len(SHARES)
+LAG = 2
 
 
 def kernel(
     n_ep, n_dp, lines, cap, cuts,
     res_any, gain_any, rwt_any, og_any, ids_any, hidt_any, w_any,
     hgt, wg, rg_ref, rgt_ref, gg_ref,
-    res_s, gain_s, rwt_s, ids_s, tok, meta, metat, hot_s, send, recv, w, hid3, hidt, inner_s, scaled, normed_s, inv_s,
+    res_s, gain_s, rwt_s, ids_s, tok, meta, metat, hot_s, send, recv, w, hid3, hidt, inner_s, scaled, normed_t, inv_s,
     prob_s, rank_s, ssend, srecv, part, rsbuf, agbuf,
-    in_sem, tok_send, tok_recv, meta_send, meta_recv, row_send, row_recv, sc_send, sc_recv, rs_send, rs_recv, ag_send, ag_recv,
+    in_sem, tok_send, tok_recv, meta_send, meta_recv, row_send, row_recv, sc_send, sc_recv, rs_send, rs_recv, ag_send, ag_recv, twin_send, twin_recv,
 ):
     n = n_ep * n_dp
     width, tokens = res_s.shape
     experts = rwt_s.shape[0]
     ff = w.shape[0]
-    pad_width = send.shape[2]
+    spare = send[0].shape[2] - cuts[0][1]
     plane = n // lines
     group = plane * cap
     pieces = len(cuts)
     owned = part.shape[0]
     me = lax.axis_index("ep") * n_dp + lax.axis_index("dp")
-    mine = (me * owned + n - 1) // n
-    owner = mine * n < (me + 1) * owned
+    half = owned // 2
+    core = me % 2
+    seat = (me // 2 * half + n // 2 - 1) // (n // 2)
+    owner = seat * (n // 2) < (me // 2 + 1) * half
+    mine = core * half + seat
     z = me // plane
     p = me % plane
 
@@ -105,7 +110,8 @@
                 c.start()
 
     ssend[...] = jnp.zeros_like(ssend)
-    part[owned - 1] = jnp.zeros(part.shape[1:], BF16)
+    for b in range(width // 128, owned):
+        part[b] = jnp.zeros(part.shape[1:], BF16)
     load_og.wait()
     neighbours = jnp.where(z > 0, 1, 0) + jnp.where(z < lines - 1, 1, 0)
     pl.semaphore_wait(barrier, plane - 1 + neighbours)
@@ -121,7 +127,7 @@
     unit = floated * inverse
     normed = (unit * gain).astype(BF16)
     inv_s[...] = inverse
-    normed_s[...] = normed
+    normed_t[...] = normed.T
     logits = jnp.dot(rwt_s[...], normed, preferred_element_type=F32)
     row_e = lax.broadcasted_iota(jnp.int32, (experts, tokens), 0)
     match = jnp.zeros((experts, tokens), F32)
@@ -173,9 +179,6 @@
             for c in along(source, i, j):
                 c.wait_recv()
 
-    def cols(j):
-        return cuts[j][0], cuts[j][1] + (pad_width - width if j == 0 else 0)
-
     def pack(j, source, i):
         first = source * plane
         lane0, lanes = cuts[j]
@@ -188,31 +191,35 @@
             hot = jnp.where(hit, F32(1.0), F32(0.0)).reshape(group, tokens).astype(BF16)
             weight = jnp.sum(jnp.where(hit, pt, F32(0.0)), -1, keepdims=True)
             hot_s[i] = hot
-            send[pl.ds(first, plane), :, pl.ds(width, pad_width - width)] = jnp.broadcast_to(
-                weight, (plane, cap, pad_width - width)
+            send[0][pl.ds(first, plane), :, pl.ds(lanes, spare)] = jnp.broadcast_to(
+                weight, (plane, cap, spare)
             ).astype(BF16)
         else:
             hot = hot_s[i]
         rows = lax.dot_general(
             hot, tok[source, pl.ds(lane0, lanes)], (((1,), (1,)), ((), ())), preferred_element_type=F32
         )
-        send[pl.ds(first, plane), :, pl.ds(lane0, lanes)] = rows.reshape(plane, cap, lanes).astype(BF16)
+        send[j][pl.ds(first, plane), :, pl.ds(0, lanes)] = rows.reshape(plane, cap, lanes).astype(BF16)
         own = first + p
-        at = pl.ds(*cols(j))
-        recv[own, :, at] = send[own, :, at]
+        recv[j][own] = send[j][own]
 
         def push(k, _):
-            row_copy(source, (p + k) % plane, p, j).start()
+            row_copy(source, partner(plane - k), p, j).start()
             return 0
 
         lax.fori_loop(1, plane, push, 0)
+
+    def partner(k):
+        if plane & (plane - 1):
+            return (p + k) % plane
+        bits = range(plane.bit_length() - 1)
+        return sum((p // (1 << b) + k // (1 << b)) % 2 * (1 << b) for b in bits)
 
     def row_copy(source, q, slot, j):
         first = source * plane
         to = z * plane + q
-        at = pl.ds(*cols(j))
         return remote(
-            send.at[first + q, :, at], recv.at[first + slot, :, at], row_send.at[0], row_recv.at[source, j],
+            send[j].at[first + q], recv[j].at[first + slot], row_send.at[j], row_recv.at[source, j],
             to // n_dp, to % n_dp,
         )
 
@@ -223,12 +230,12 @@
         first = source * plane
         lane0, lanes = cuts[j]
 
-        landed = recv.at[pl.ds(first, plane - 1), :, pl.ds(*cols(j))]
-        all_of(landed, row_send.at[0], row_recv.at[source, j]).wait_recv()
+        landed = recv[j].at[pl.ds(first, plane - 1)]
+        all_of(landed, row_send.at[j], row_recv.at[source, j]).wait_recv()
         at = pl.ds(pl.multiple_of(first * cap, group), group)
-        tail = recv[pl.ds(first, plane), :, pl.ds(pad_width - 128, 128)].astype(F32).reshape(group, 128)
-        weight = tail[:, width - pad_width + 128 : width - pad_width + 129]
-        grad = recv[pl.ds(first, plane), :, pl.ds(lane0, lanes)].astype(F32).reshape(group, lanes)
+        tail = recv[0][pl.ds(first, plane), :, pl.ds(cuts[0][1] + spare - 128, 128)].astype(F32).reshape(group, 128)
+        weight = tail[:, 128 - spare : 129 - spare]
+        grad = recv[j][pl.ds(first, plane), :, pl.ds(0, lanes)].astype(F32).reshape(group, lanes)
         inner = lax.dot_general(
             w[:, lane0 : lane0 + lanes], grad.astype(BF16), (((1,), (1,)), ((), ())), preferred_element_type=F32
         )
@@ -281,7 +288,7 @@
             def _(j=j, later=later):
                 sides(later, functools.partial(relay, (j + 1) % pieces))
 
-            if j == min(1, pieces - 1):
+            if j == min(LAG, pieces - 1):
                 @pl.when(k == 0)
                 def _():
                     load_h.wait()
@@ -289,10 +296,7 @@
                         hid3[i] = hidt[:, i * group : (i + 1) * group]
                     load_w.wait()
 
-            if j > 0:
-                sides(k, functools.partial(chunk, j - 1))
-            else:
-                sides(k - 1, functools.partial(chunk, pieces - 1))
+            sides(k + (j - LAG) // pieces, functools.partial(chunk, (j - LAG) % pieces))
         return 0
 
     lax.fori_loop(0, lines + 1, stage, 0)
@@ -304,14 +308,6 @@
         at = pl.ds(pl.multiple_of(b * rows_of, rows_of), rows_of)
         wg[at] = jnp.dot(hidt[at], scaled[...], preferred_element_type=F32).astype(BF16)
         return 0
-
-    def others(fn):
-        def step(i, _):
-            @pl.when(i != me)
-            def _():
-                fn(i)
-            return 0
-        lax.fori_loop(0, n, step, 0)
 
     cut1, cut2 = (2 * blocks) // 5, (4 * blocks) // 5
     lax.fori_loop(0, cut1, wg_block, 0)
@@ -326,24 +322,28 @@
     lg = prob * (score - jnp.sum(prob * score, 0, keepdims=True))
     hi = lg.astype(BF16)
     lo = (lg - hi.astype(F32)).astype(BF16)
-    both = lax.dot_general(
-        jnp.concatenate([hi, lo], 0), normed_s[...], (((1,), (1,)), ((), ())),
-        preferred_element_type=F32,
-    )
+    both = jnp.dot(jnp.concatenate([hi, lo], 0), normed_t[...], preferred_element_type=F32)
     router = (both[:experts] + both[experts:]).astype(BF16)
-    for b in range(owned):
+    for b in range(-(-width // 128)):
         lanes = min(128, width - b * 128)
         part[b, :, pl.ds(0, lanes)] = router[:, b * 128 : b * 128 + lanes]
 
-    def share(b, _):
-        to = b * n // owned
-
-        @pl.when(to != me)
-        def _():
-            remote(part.at[b], rsbuf.at[me], rs_send.at[0], rs_recv.at[0], to // n_dp, to % n_dp).start()
-        return 0
-
-    lax.fori_loop(0, owned, share, 0)
+    def scatter(order):
+        for at in order:
+            to = at // 2 * (n // 2) // half * 2 + at % 2
+            b = at % 2 * half + at // 2
+
+            @pl.when(to != me)
+            def _(to=to, b=b):
+                remote(part.at[b], rsbuf.at[me], rs_send.at[0], rs_recv.at[0], to // n_dp, to % n_dp).start()
+
+    @pl.when(z < lines // 2)
+    def _():
+        scatter(range(owned - 1, -1, -1))
+
+    @pl.when(z >= lines // 2)
+    def _():
+        scatter(range(owned))
 
     @pl.when(owner)
     def _():
@@ -355,7 +355,18 @@
     def _():
         all_of(rsbuf.at[pl.ds(0, n - 1)], rs_send.at[0], rs_recv.at[0]).wait_recv()
         agbuf[mine] = jnp.sum(rsbuf[...].astype(F32), 0).astype(BF16)
-        others(lambda i: remote(agbuf.at[mine], agbuf.at[mine], ag_send.at[0], ag_recv.at[0], i // n_dp, i % n_dp).start())
+
+        def spread(k, _):
+            i = jnp.where(z < lines // 2, n // 2 - 1 - k, k) * 2 + core
+
+            @pl.when(i != me)
+            def _():
+                remote(
+                    agbuf.at[mine], agbuf.at[mine], ag_send.at[0], ag_recv.at[0], i // n_dp, i % n_dp
+                ).start()
+            return 0
+
+        lax.fori_loop(0, n // 2, spread, 0)
 
     rwt = rwt_s[...]
     ngrad = lax.dot_general(
@@ -369,7 +380,8 @@
 
     lax.fori_loop(cut2, blocks, wg_block, 0)
 
-    all_of(send.at[pl.ds(0, lines * (plane - 1))], row_send.at[0], row_recv.at[0, 0]).wait_send()
+    for j in range(pieces):
+        all_of(send[j].at[pl.ds(0, lines * (plane - 1))], row_send.at[j], row_recv.at[0, j]).wait_send()
 
     def finish_toks(source, _):
         def sent(side):
@@ -395,15 +407,21 @@
     @pl.when(owner)
     def _():
         all_of(part.at[pl.ds(0, owned - 1)], rs_send.at[0], rs_recv.at[0]).wait_send()
-        all_of(agbuf.at[pl.ds(0, owned - 1)], ag_send.at[0], ag_recv.at[0]).wait_recv()
+        all_of(agbuf.at[pl.ds(0, half - 1)], ag_send.at[0], ag_recv.at[0]).wait_recv()
 
     @pl.when(jnp.logical_not(owner))
     def _():
-        all_of(part.at[pl.ds(0, owned)], rs_send.at[0], rs_recv.at[0]).wait_send()
-        all_of(agbuf.at[pl.ds(0, owned)], ag_send.at[0], ag_recv.at[0]).wait_recv()
+        all_of(part, rs_send.at[0], rs_recv.at[0]).wait_send()
+        all_of(agbuf.at[pl.ds(0, half)], ag_send.at[0], ag_recv.at[0]).wait_recv()
+
+    to = me + 1 - 2 * core
+    ours = agbuf.at[pl.ds(core * half, half)]
+    twin = remote(ours, ours, twin_send.at[0], twin_recv.at[0], to // n_dp, to % n_dp)
+    twin.start()
+    twin.wait_recv()
 
     gain_row = gain_s[...].reshape(1, width)
-    for b in range(owned):
+    for b in range(-(-width // 128)):
         lanes = min(128, width - b * 128)
         at = slice(b * 128, b * 128 + lanes)
         total = agbuf[b, :, pl.ds(0, lanes)].astype(F32)
@@ -413,7 +431,9 @@
 
     @pl.when(owner)
     def _():
-        all_of(rsbuf.at[pl.ds(0, n - 1)], ag_send.at[0], ag_recv.at[0]).wait_send()
+        all_of(rsbuf.at[pl.ds(0, n // 2 - 1)], ag_send.at[0], ag_recv.at[0]).wait_send()
+
+    twin.wait_send()
 
 
 def store(hgt, wg, rg, rgt, gg, hgt_any, wg_any, rg_any, rgt_any, gg_any, sem):
@@ -436,9 +456,10 @@
         c.wait()
 
 
-def column_cuts(width, pad_width, count):
+def column_cuts(width, pad_width):
     tiles = pad_width // 128
-    sizes = [tiles // count + (1 if i < tiles % count else 0) for i in range(count)]
+    ends = [tiles * sum(SHARES[: i + 1]) // sum(SHARES) for i in range(PIECES)]
+    sizes = [e - b for b, e in zip([0] + ends, ends)]
     last = (tiles - sizes[0]) * 128
     cuts = [(last, width - last)]
     at = 0
@@ -466,9 +487,12 @@
     rows = experts * cap
     plane = n // lines
     group = plane * cap
-    owned = -(-width // 128)
+    owned = -(-width // 256) * 2
     assert owned <= n
-    cuts = column_cuts(width, pad_width, PIECES)
+    cuts = column_cuts(width, pad_width)
+    rows_of_piece = [
+        pltpu.VMEM((n, cap, lanes + (pad_width - width if j == 0 else 0)), BF16) for j, (_, lanes) in enumerate(cuts)
+    ]
     vmem = pl.BlockSpec(memory_space=pltpu.VMEM)
     anyspace = pl.BlockSpec(memory_space=pl.ANY)
     dma = pltpu.SemaphoreType.DMA
@@ -491,14 +515,14 @@
             pltpu.VMEM((lines, 2 * experts, tokens), BF16),
             pltpu.VMEM((2 * experts, 1, tokens), F32),
             pltpu.VMEM((2, group, tokens), BF16),
-            pltpu.VMEM((n, cap, pad_width), BF16),
-            pltpu.VMEM((n, cap, pad_width), BF16),
+            rows_of_piece,
+            rows_of_piece,
             pltpu.VMEM((ff, width), BF16),
             pltpu.VMEM((lines, ff, group), BF16),
             pltpu.VMEM((ff, rows), BF16),
             pltpu.VMEM((2, ff, group), F32),
             pltpu.VMEM((rows, width), BF16),
-            pltpu.VMEM((width, tokens), BF16),
+            pltpu.VMEM((tokens, width), BF16),
             pltpu.VMEM((1, tokens), F32),
             pltpu.VMEM((experts, tokens), F32),
             pltpu.VMEM((experts, tokens), F32),
@@ -509,8 +533,8 @@
             pltpu.VMEM((owned, experts, 128), BF16),
             dma((7,)),
             dma((lines, 2)), dma((lines, PIECES)), dma((lines, 2)), dma((lines,)),
-            dma((1,)), dma((lines, PIECES)), dma((1,)), dma((1,)),
-            dma((1,)), dma((1,)), dma((1,)), dma((1,)),
+            dma((PIECES,)), dma((lines, PIECES)), dma((1,)), dma((1,)),
+            dma((1,)), dma((1,)), dma((1,)), dma((1,)), dma((1,)), dma((1,)),
         ],
         compiler_params=pltpu.CompilerParams(
             collective_id=0, has_side_effects=True, vmem_limit_bytes=53_000_000

time: 84.9 us -> 82.8 us (0.975)
  Pallas kernels: 84.1 us -> 82 us
    pallas_call x1, Pallas kernels: 79.8 us -> 77.6 us  [on_device(): pl.pallas_call(functools.partial(kernel, n_ep, n_dp, lines, cap, cuts), o...]
where the time goes in v2:
time: 82.8 us; the launch traced here: 82.7 us
  Pallas kernels  82 us (99%)
    pallas_call x1, Pallas kernels, on_device(): pl.pallas_call(functools.partial(kernel, n_ep, n_dp, lines, cap, cuts), o...  77.6 us
    pallas_call x1, Pallas kernels, on_device(): pl.pallas_call(store, out_shape=tuple((jax.ShapeDtypeStruct(s, t) for s,...  4.39 us

profile of v2, /device:TPU:0, one launch (start us, length us, event | category | flops | bytes accessed | tf_op | source)
XLA Modules:
  0.0 82.7 jit_solution(260531370700173035)
XLA Ops:
  0.6 77.6 %expert_backward.1 = (bf16[1440,768]{1,0:T(8,128)(2,1)S(1)}, bf16[1440,2880]{1,0:T(8,128)(2,1)S(1)}, bf16[2880,128]{1,0:T(8,128)(2,1)S(1)}, f32[32,2880]{1,0:T(8,128)S(1)}, f32[1,2880]{1,0:T(1,128)S(1)}) custom-call(bf16[2880,128]{1,0:T(8,128)(2,1)} %bitcast.16, f32[2880]{0:T(1024)} %gain_any.1, bf16[32,2880]{1,0:T(8,128)(2,1)} %bitcast.18, ...), custom_call_target="tpu_custom_call" | custom-call | tf_op jit(solution)/shard_map/expert_backward/pallas_call | solution.py:504
  78.3 4.4 %store.1 = (bf16[1440,768]{1,0:T(8,128)(2,1)}, bf16[1440,2880]{1,0:T(8,128)(2,1)}, bf16[2880,128]{1,0:T(8,128)(2,1)}, f32[32,2880]{1,0:T(8,128)}, f32[2880]{0:T(1024)}) custom-call(bf16[1440,768]{1,0:T(8,128)(2,1)S(1)} %get-tuple-element.15.hgt, bf16[1440,2880]{1,0:T(8,128)(2,1)S(1)} %get-tuple-element.16.wg, bf16[2880,128]{1,0:T(8,128)(2,1)S(1)} %get-tuple-element.17.rg, ...), custom_call_target="tpu_custom_call" | custom-call | tf_op jit(solution)/shard_map/store/pallas_call | solution.py:544

commit v3 on v2

--- a/solution.py
+++ b/solution.py
@@ -20,7 +20,7 @@
     n_ep, n_dp, lines, cap, cuts,
     res_any, gain_any, rwt_any, og_any, ids_any, hidt_any, w_any,
     hgt, wg, rg_ref, rgt_ref, gg_ref,
-    res_s, gain_s, rwt_s, ids_s, tok, meta, metat, hot_s, send, recv, w, hid3, hidt, inner_s, scaled, normed_t, inv_s,
+    res_s, gain_s, rwt_s, ids_s, tok, meta, hot_s, send, recv, w, hid3, hidt, inner_s, scaled, normed_t, inv_s,
     prob_s, rank_s, ssend, srecv, part, rsbuf, agbuf,
     in_sem, tok_send, tok_recv, meta_send, meta_recv, row_send, row_recv, sc_send, sc_recv, rs_send, rs_recv, ag_send, ag_recv, twin_send, twin_recv,
 ):
@@ -143,7 +143,18 @@
     rank = jnp.where(match > 0, rank, F32(-1.0))
     prob_s[...] = prob
     rank_s[...] = rank
-    meta[z] = jnp.concatenate([rank, prob], 0).astype(BF16)
+    topk = ids.shape[0]
+
+    def chosen(values):
+        return [
+            jnp.sum(jnp.where(ids[k : k + 1, :] == row_e, values, F32(0.0)), 0, keepdims=True) for k in range(topk)
+        ]
+
+    unused = meta.shape[1] - 3 * topk
+    info = [ids.astype(F32)] + chosen(rank) + chosen(prob)
+    if unused:
+        info.append(jnp.zeros((unused, tokens), F32))
+    meta[z] = jnp.concatenate(info, 0).astype(BF16)
 
     for side in range(2):
         to_side(side, [meta_copy(z, side)])
@@ -183,9 +194,14 @@
         first = source * plane
         lane0, lanes = cuts[j]
         if j == 0:
-            metat[...] = meta[source].astype(F32).reshape(2 * experts, 1, tokens)
-            rt = metat[pl.ds(z * plane, plane)]
-            pt = metat[pl.ds(experts + z * plane, plane)]
+            info = meta[source].astype(F32)
+            expert = (lax.broadcasted_iota(jnp.int32, (plane, 1, tokens), 0) + z * plane).astype(F32)
+            rt = jnp.full((plane, 1, tokens), -1.0, F32)
+            pt = jnp.zeros((plane, 1, tokens), F32)
+            for k in range(topk):
+                here = expert == info[k : k + 1].reshape(1, 1, tokens)
+                rt = jnp.where(here, info[topk + k : topk + k + 1].reshape(1, 1, tokens), rt)
+                pt = jnp.where(here, info[2 * topk + k : 2 * topk + k + 1].reshape(1, 1, tokens), pt)
             slot = lax.broadcasted_iota(jnp.int32, (plane, cap, tokens), 1).astype(F32)
             hit = slot == rt
             hot = jnp.where(hit, F32(1.0), F32(0.0)).reshape(group, tokens).astype(BF16)
@@ -203,11 +219,15 @@
         own = first + p
         recv[j][own] = send[j][own]
 
-        def push(k, _):
-            row_copy(source, partner(plane - k), p, j).start()
-            return 0
-
-        lax.fori_loop(1, plane, push, 0)
+        if plane > 8:
+            def push(k, _):
+                row_copy(source, partner(plane - k), p, j).start()
+                return 0
+
+            lax.fori_loop(1, plane, push, 0)
+        else:
+            for k in range(1, plane):
+                row_copy(source, partner(plane - k), p, j).start()
 
     def partner(k):
         if plane & (plane - 1):
@@ -512,8 +532,7 @@
             pltpu.VMEM((experts, width), BF16),
             pltpu.VMEM((topk, tokens), jnp.int32),
             pltpu.VMEM((lines, width, tokens), BF16),
-            pltpu.VMEM((lines, 2 * experts, tokens), BF16),
-            pltpu.VMEM((2 * experts, 1, tokens), F32),
+            pltpu.VMEM((lines, -(-3 * topk // 16) * 16, tokens), BF16),
             pltpu.VMEM((2, group, tokens), BF16),
             rows_of_piece,
             rows_of_piece,

time: 82.8 us -> 81.9 us (0.989)
  Pallas kernels: 82 us -> 81.1 us
    pallas_call x1, Pallas kernels: 77.6 us -> 76.7 us  [on_device(): pl.pallas_call(functools.partial(kernel, n_ep, n_dp, lines, cap, cuts), o...]
where the time goes in v3:
time: 81.9 us; the launch traced here: 81.8 us
  Pallas kernels  81.1 us (99%)
    pallas_call x1, Pallas kernels, on_device(): pl.pallas_call(functools.partial(kernel, n_ep, n_dp, lines, cap, cuts), o...  76.7 us
    pallas_call x1, Pallas kernels, on_device(): pl.pallas_call(store, out_shape=tuple((jax.ShapeDtypeStruct(s, t) for s,...  4.39 us

profile of v3, /device:TPU:0, one launch (start us, length us, event | category | flops | bytes accessed | tf_op | source)
XLA Modules:
  0.0 81.8 jit_solution(5398425393736382897)
XLA Ops:
  0.6 76.7 %expert_backward.1 = (bf16[1440,768]{1,0:T(8,128)(2,1)S(1)}, bf16[1440,2880]{1,0:T(8,128)(2,1)S(1)}, bf16[2880,128]{1,0:T(8,128)(2,1)S(1)}, f32[32,2880]{1,0:T(8,128)S(1)}, f32[1,2880]{1,0:T(1,128)S(1)}) custom-call(bf16[2880,128]{1,0:T(8,128)(2,1)} %bitcast.16, f32[2880]{0:T(1024)} %gain_any.1, bf16[32,2880]{1,0:T(8,128)(2,1)} %bitcast.18, ...), custom_call_target="tpu_custom_call" | custom-call | tf_op jit(solution)/shard_map/expert_backward/pallas_call | solution.py:524
  77.4 4.4 %store.1 = (bf16[1440,768]{1,0:T(8,128)(2,1)}, bf16[1440,2880]{1,0:T(8,128)(2,1)}, bf16[2880,128]{1,0:T(8,128)(2,1)}, f32[32,2880]{1,0:T(8,128)}, f32[2880]{0:T(1024)}) custom-call(bf16[1440,768]{1,0:T(8,128)(2,1)S(1)} %get-tuple-element.15.hgt, bf16[1440,2880]{1,0:T(8,128)(2,1)S(1)} %get-tuple-element.16.wg, bf16[2880,128]{1,0:T(8,128)(2,1)S(1)} %get-tuple-element.17.rg, ...), custom_call_target="tpu_custom_call" | custom-call | tf_op jit(solution)/shard_map/store/pallas_call | solution.py:563

commit v4 on v3

--- a/solution.py
+++ b/solution.py
@@ -342,11 +342,7 @@
     lg = prob * (score - jnp.sum(prob * score, 0, keepdims=True))
     hi = lg.astype(BF16)
     lo = (lg - hi.astype(F32)).astype(BF16)
-    both = jnp.dot(jnp.concatenate([hi, lo], 0), normed_t[...], preferred_element_type=F32)
-    router = (both[:experts] + both[experts:]).astype(BF16)
-    for b in range(-(-width // 128)):
-        lanes = min(128, width - b * 128)
-        part[b, :, pl.ds(0, lanes)] = router[:, b * 128 : b * 128 + lanes]
+    stacked = jnp.concatenate([hi, lo], 0)
 
     def scatter(order):
         for at in order:
@@ -357,13 +353,22 @@
             def _(to=to, b=b):
                 remote(part.at[b], rsbuf.at[me], rs_send.at[0], rs_recv.at[0], to // n_dp, to % n_dp).start()
 
-    @pl.when(z < lines // 2)
-    def _():
-        scatter(range(owned - 1, -1, -1))
-
-    @pl.when(z >= lines // 2)
-    def _():
-        scatter(range(owned))
+    for side in range(2):
+        first = side * half * 128
+        lanes = min(width - first, half * 128)
+        both = jnp.dot(stacked, normed_t[:, first : first + lanes], preferred_element_type=F32)
+        router = (both[:experts] + both[experts:]).astype(BF16)
+        for t in range(-(-lanes // 128)):
+            end = min(t * 128 + 128, lanes)
+            part[side * half + t, :, pl.ds(0, end - t * 128)] = router[:, t * 128 : end]
+
+        @pl.when(z < lines // 2)
+        def _(side=side):
+            scatter(range(owned - 2 + side, -1, -2))
+
+        @pl.when(z >= lines // 2)
+        def _(side=side):
+            scatter(range(side, owned, 2))
 
     @pl.when(owner)
     def _():

time: 81.9 us -> 82.1 us (level)
  no operation moved by 1% of the time
where the time goes in v4:
time: 82.1 us; the launch traced here: 82 us
  Pallas kernels  81.3 us (99%)
    pallas_call x1, Pallas kernels, on_device(): pl.pallas_call(functools.partial(kernel, n_ep, n_dp, lines, cap, cuts), o...  76.9 us
    pallas_call x1, Pallas kernels, on_device(): pl.pallas_call(store, out_shape=tuple((jax.ShapeDtypeStruct(s, t) for s,...  4.39 us

profile of v4, /device:TPU:0, one launch (start us, length us, event | category | flops | bytes accessed | tf_op | source)
XLA Modules:
  0.0 82.0 jit_solution(13830545618170609041)
XLA Ops:
  0.6 76.9 %expert_backward.1 = (bf16[1440,768]{1,0:T(8,128)(2,1)S(1)}, bf16[1440,2880]{1,0:T(8,128)(2,1)S(1)}, bf16[2880,128]{1,0:T(8,128)(2,1)S(1)}, f32[32,2880]{1,0:T(8,128)S(1)}, f32[1,2880]{1,0:T(1,128)S(1)}) custom-call(bf16[2880,128]{1,0:T(8,128)(2,1)} %bitcast.16, f32[2880]{0:T(1024)} %gain_any.1, bf16[32,2880]{1,0:T(8,128)(2,1)} %bitcast.18, ...), custom_call_target="tpu_custom_call" | custom-call | tf_op jit(solution)/shard_map/expert_backward/pallas_call | solution.py:529
  77.6 4.4 %store.1 = (bf16[1440,768]{1,0:T(8,128)(2,1)}, bf16[1440,2880]{1,0:T(8,128)(2,1)}, bf16[2880,128]{1,0:T(8,128)(2,1)}, f32[32,2880]{1,0:T(8,128)}, f32[2880]{0:T(1024)}) custom-call(bf16[1440,768]{1,0:T(8,128)(2,1)S(1)} %get-tuple-element.15.hgt, bf16[1440,2880]{1,0:T(8,128)(2,1)S(1)} %get-tuple-element.16.wg, bf16[2880,128]{1,0:T(8,128)(2,1)S(1)} %get-tuple-element.17.rg, ...), custom_call_target="tpu_custom_call" | custom-call | tf_op jit(solution)/shard_map/store/pallas_call | solution.py:568
